TPU v7x, 256 devices: a whole 4x4x8 slice. The times are simulated.
256 devices in a mesh: span: 16 (over y, x), model: 16 (over z, core).
Axes of the slice: x: 4, y: 4, z: 8, core: 2. Of those that a mesh axis runs over, the one named last changes fastest.
Arguments:
- latents: bfloat16 [16, 8192, 512], P(None, ('span', 'model')), may hold values from -6 to 6
- rotary_rows: bfloat16 [16, 8192, 64], P(None, ('span', 'model')), may hold values from -6 to 6
- latent_gain: float32 [512], replicated, may hold values from 0.25 to 1.75
- key_up: bfloat16 [512, 16, 128], P(None, 'model'), may hold values from -0.25 to 0.25
- value_up: bfloat16 [512, 16, 128], P(None, 'model'), may hold values from -0.25 to 0.25
Outputs:
- decode_keys: bfloat16 [16, 16, 192, 8192], P('span', 'model')
- decode_values: bfloat16 [16, 8192, 16, 128], P('span', None, 'model')
All inputs are finite; a program needn't handle non-finite values.
Results may differ from a plain program's by a relative error of at most 0.0049.
Values may be sent and summed in bfloat16 or wider, within the bound.
A program may use at most 64 MiB of HBM per device.

v0:
```python
import jax
import jax.numpy as jnp
from jax import lax
from jax.sharding import PartitionSpec as P


def sent_together(arrays, axis, split_dim, concat_dim, along):
    both = jnp.concatenate(arrays, axis=along)
    whole, at, outs = (
        lax.all_to_all(both, axis, split_axis=split_dim, concat_axis=concat_dim, tiled=True),
        0,
        [],
    )
    for a in arrays:
        outs.append(lax.slice_in_dim(whole, at, at + a.shape[along], axis=along))
        at += a.shape[along]
    return tuple(outs)


def in_one_piece(arrays, axis, dim, along):
    ends, at = ([], 0)
    for a in arrays[:-1]:
        at += a.shape[along]
        ends.append(at)
    both = jnp.concatenate(arrays, axis=along)
    return tuple(jnp.split(lax.all_gather(both, axis, axis=dim, tiled=True), ends, axis=along))


def widen_rows(rows, rotary, key_up, value_up):
    wide_keys = jnp.einsum(
        "btr,rhk->bthk", rows, key_up, preferred_element_type=jnp.float32
    ).astype(jnp.bfloat16)
    shared = rotary[:, :, None]
    wide_values = jnp.einsum(
        "btr,rhk->bthk", rows, value_up, preferred_element_type=jnp.float32
    ).astype(jnp.bfloat16)
    return (jnp.concatenate([wide_keys, shared], axis=-1), wide_values)


def scale_rows(vectors, row_gain):
    return (
        vectors * lax.rsqrt(jnp.mean(vectors * vectors, axis=-1, keepdims=True) + 1e-06) * row_gain
    )


def shards(latents, rotary_rows, latent_gain, key_up, value_up):
    rows_ready = scale_rows(latents.astype(jnp.float32), latent_gain).astype(jnp.bfloat16)
    rows_moved, rotary_moved = sent_together((rows_ready, rotary_rows), "span", 0, 1, 2)
    rows_cut = rows_moved.reshape(
        rows_moved.shape[0], lax.axis_size("span"), -1, rows_moved.shape[2]
    )
    rotary_cut = rotary_moved.reshape(
        rotary_moved.shape[0], lax.axis_size("span"), -1, rotary_moved.shape[2]
    )
    rows_joined, rotary_joined = in_one_piece((rows_cut, rotary_cut), "model", 2, 3)
    rows_whole = rows_joined.reshape(rows_joined.shape[0], -1, rows_joined.shape[3])
    rotary_whole = rotary_joined.reshape(rotary_joined.shape[0], -1, rotary_joined.shape[3])
    decode_keys, decode_values = widen_rows(rows_whole, rotary_whole, key_up, value_up)
    decode_keys = jnp.transpose(decode_keys, (0, 2, 3, 1))
    return (decode_keys, decode_values)


def solution(mesh):
    placed = (
        P(None, ("span", "model"), None),
        P(None, ("span", "model"), None),
        P(),
        P(None, "model", None),
        P(None, "model", None),
    )
    return jax.shard_map(
        shards,
        mesh=mesh,
        in_specs=placed,
        out_specs=(P("span", "model", None, None), P("span", None, "model", None)),
        check_vma=False,
    )
```

profile of v0, /device:TPU:1, one launch (start us, length us, event | category | flops | bytes accessed | tf_op | source)
XLA Modules:
  0.0 126.5 jit_solution(15320738110184125688)
XLA Ops:
  7.2 0.0 copy-start
  7.2 0.0 all-gather.2.cloned.1.call-start
  7.2 1.2 fusion.2
  8.5 1.2 fusion.4
  9.7 1.0 pad_maximum_fusion
  10.7 19.2 %all_to_all.12 = bf16[16,32,576]{2,1,0:T(8,128)(2,1)S(1)} all-to-all(bf16[16,32,576]{2,1,0:T(8,128)(2,1)S(1)} %pad_maximum_fusion), channel_id=1, replica_groups=mesh['span'=16,'model'=16] {'span'}, dimensions={0} | all-to-all | bytes 1179648 | tf_op jit(solution)/shard_map/all_to_all | solution.py:10
  30.0 0.9 pad_maximum_fusion.1
  30.9 0.0 all-gather.2.cloned.1.call-update
  30.9 66.9 %all-gather.2.cloned.1.call-done = bf16[1,16,512,576]{3,2,1,0:T(8,128)(2,1)} async-done(((bf16[1,16,32,576]{3,2,1,0:T(8,128)(2,1)}), bf16[1,16,512,576]{3,2,1,0:T(8,128)(2,1)}) %all-gather.2.cloned.1.call-update) | async-done | bytes 9437200 | tf_op jit(solution)/shard_map/all_gather | solution.py:26
  97.8 0.0 slice-start
  97.8 1.6 %slice-done = bf16[1,16,512,64]{3,2,1,0:T(8,128)(2,1)S(1)} async-done(((bf16[1,16,512,576]{3,2,1,0:T(8,128)(2,1)}), bf16[1,16,512,64]{3,2,1,0:T(8,128)(2,1)S(1)}, s32[]{:S(2)}) %slice-start) | async-done | bytes 1048600 | tf_op jit(solution)/shard_map/split | solution.py:26
  99.4 0.8 copy.10
  100.2 7.4 %split.8 = bf16[1,16,512,512]{3,2,1,0:T(8,128)(2,1)} slice(bf16[1,16,512,576]{3,2,1,0:T(8,128)(2,1)} %all-gather.2.cloned.1.call-done), slice={[0:1], [0:16], [0:512], [0:512]} | slice | bytes 16777216 | tf_op jit(solution)/shard_map/split | solution.py:26
  107.6 0.0 copy-done
  107.6 0.0 copy-start.1
  107.7 0.0 copy-start.2
  107.7 6.4 %fusion = bf16[1,8192,1,128]{1,3,2,0:T(8,128)(2,1)S(1)} fusion(bf16[8192,512]{1,0:T(8,128)(2,1)} %bitcast.19, bf16[512,1,128]{2,0,1:T(8,128)(2,1)S(1)} %copy-done), kind=kOutput, calls=%fused_computation.2 | convolution fusion | flops 1074790400 | bytes 10616832 | tf_op jit(solution)/shard_map/btr,rhk->bthk/dot_general | solution.py:30
  114.0 0.0 copy-done.1
  114.0 0.0 copy-done.2
  114.0 3.7 %fusion.1 = bf16[1,8192,1,128]{3,1,2,0:T(8,128)(2,1)} fusion(bf16[8192,512]{1,0:T(8,128)(2,1)S(1)} %bitcast.20, bf16[512,1,128]{2,0,1:T(8,128)(2,1)S(1)} %copy-done.2), kind=kOutput, calls=%fused_computation.3 | convolution fusion | flops 1074790400 | bytes 10616832 | tf_op jit(solution)/shard_map/btr,rhk->bthk/dot_general | solution.py:34
  117.7 1.9 %maximum_bitcast_fusion = bf16[1,1,192,8192]{3,2,1,0:T(8,128)(2,1)} fusion(bf16[1,8192,1,64]{1,3,2,0:T(8,128)(2,1)S(1)} %copy.10, bf16[1,8192,1,128]{1,3,2,0:T(8,128)(2,1)S(1)} %fusion), kind=kLoop, calls=%fused_computation.4 | loop fusion | flops 6291456 | bytes 6291456 | tf_op jit(solution)/shard_map/transpose | solution.py:59
  (3 shorter events, 0.1 us)
Async XLA Ops:
  7.2 100.5 %copy-start = (bf16[512,1,128]{2,0,1:T(8,128)(2,1)S(1)}, bf16[512,1,128]{2,0,1:T(8,128)(2,1)}, u32[]{:S(2)}) copy-start(bf16[512,1,128]{2,0,1:T(8,128)(2,1)} %param.8) | copy-start | bytes 393220
  7.2 90.6 %all-gather.2.cloned.1.call-start = ((), (), s32[]{:S(2)}) async-start(), calls=%async_computation.1 | async-start | bytes 11141120 | tf_op jit(solution)/shard_map/all_gather | solution.py:26
  97.8 1.6 %slice-start = ((bf16[1,16,512,576]{3,2,1,0:T(8,128)(2,1)}), bf16[1,16,512,64]{3,2,1,0:T(8,128)(2,1)S(1)}, s32[]{:S(2)}) async-start(bf16[1,16,512,576]{3,2,1,0:T(8,128)(2,1)} %all-gather.2.cloned.1.call-done), calls=%async_computation.2 | async-start | bytes 4194304 | tf_op jit(solution)/shard_map/split | solution.py:26
  107.6 6.4 %copy-start.1 = (bf16[1,16,512,512]{3,2,1,0:T(8,128)(2,1)S(1)}, bf16[1,16,512,512]{3,2,1,0:T(8,128)(2,1)}, u32[]{:S(2)}) copy-start(bf16[1,16,512,512]{3,2,1,0:T(8,128)(2,1)} %split.8) | copy-start | bytes 25165828
  107.7 6.4 %copy-start.2 = (bf16[512,1,128]{2,0,1:T(8,128)(2,1)S(1)}, bf16[512,1,128]{2,0,1:T(8,128)(2,1)}, u32[]{:S(2)}) copy-start(bf16[512,1,128]{2,0,1:T(8,128)(2,1)} %param.9) | copy-start | bytes 393220
Sparse Core Ops, SparseCore 0:
  31.0 66.6 all-gather.1
where the time goes:
time: 127 us
  waiting for transfers between devices  66.9 us (53%)
  blocking collectives  19.2 us (15%)
  between operations  14.1 us (11%)
  matrix products  10 us (8%)
  local copies, waits for them, and re-layouts  9.92 us (8%)
  other arithmetic  6.3 us (5%)
    all_gather x1, waiting for transfers between devices, in_one_piece(): lax.all_gather(both, axis, axis=dim, tiled=True)  66.9 us
    all_to_all x1, blocking collectives, sent_together(): lax.all_to_all(both, axis, split_axis=split_dim, concat_axis=concat_dim,...  19.2 us
    split x3, local copies, waits for them, and re-layouts, in_one_piece(): jnp.split(lax.all_gather(both, axis, axis=dim, tiled=True), ends, axis=al...  9.04 us
    dot_general x1, matrix products, widen_rows(): jnp.einsum('btr,rhk->bthk', rows, key_up, preferred_element_type=jnp.floa...  6.36 us
    dot_general x1, matrix products, widen_rows(): jnp.einsum('btr,rhk->bthk', rows, value_up, preferred_element_type=jnp.fl...  3.66 us
  transfers between devices with their start and end apart: 1, of which 1 were waited for; matrix products, arithmetic and copies ran while one was open for 0% of the time, Pallas kernels for 0%

commit v1 on v0

v1 whole, which is shorter than its diff:
```python
import functools

import jax
import jax.numpy as jnp
from jax import lax
from jax.experimental import pallas as pl
from jax.experimental.pallas import tpu as pltpu
from jax.sharding import PartitionSpec as P

MESH = pl.DeviceIdType.MESH
LAG = 2
LANES = 128


def tile_of(blocks, gain_ref, wk_ref, wv_ref, groups, wide):
    depth = groups * LANES
    x = [
        jnp.concatenate([b[g * wide : (g + 1) * wide] for b in blocks], axis=0).astype(jnp.float32)
        for g in range(groups)
    ]
    squares = functools.reduce(lambda a, b: a + b, [v * v for v in x])
    scale = lax.rsqrt(jnp.sum(squares, axis=-1, keepdims=True) / depth + 1e-06)
    rows = jnp.concatenate(
        [
            (x[g] * scale * gain_ref[:, g * LANES : (g + 1) * LANES]).astype(jnp.bfloat16)
            for g in range(groups)
        ],
        axis=1,
    )
    values = jnp.dot(rows, wv_ref[...], preferred_element_type=jnp.float32).astype(jnp.bfloat16)
    keys = lax.dot_general(
        wk_ref[...], rows, (((1,), (1,)), ((), ())), preferred_element_type=jnp.float32
    ).astype(jnp.bfloat16)
    turned = []
    for b in blocks:
        packed = b[groups * wide :].astype(jnp.float32)
        turned.append(packed)
        turned.append(pltpu.roll(packed, LANES // 2, 1))
    both = jnp.concatenate(turned, axis=0).astype(jnp.bfloat16)
    eye = (
        lax.broadcasted_iota(jnp.int32, (LANES // 2, LANES), 0)
        == lax.broadcasted_iota(jnp.int32, (LANES // 2, LANES), 1)
    ).astype(jnp.bfloat16)
    rotary = lax.dot_general(
        eye, both, (((1,), (1,)), ((), ())), preferred_element_type=jnp.float32
    ).astype(jnp.bfloat16)
    return keys, rotary, values


def exchange(
    lat_hbm, rot_hbm, gain_hbm, wk_hbm, wv_hbm,
    keys_ref, values_ref,
    pack, rows, rot, gain, wk, wv, wkt,
    in_sems, own_sem, a_send, z_send, c_send, a_recv, p_recv, m_recv, cown_recv, cp_recv, cm_recv,
):
    span, model = lax.axis_index("span"), lax.axis_index("model")
    z, c = model // 2, lax.rem(model, 2)
    up = lax.rem(model + 2, 16)
    down = lax.rem(model + 14, 16)
    other = model + 1 - 2 * c
    wide = lat_hbm.shape[1]
    groups = lat_hbm.shape[2] // LANES

    barrier = pltpu.get_barrier_semaphore()
    for k in range(1, 16):
        pl.semaphore_signal(barrier, inc=1, device_id=(span ^ k, model), device_id_type=MESH)
    for m in (up, down, other):
        pl.semaphore_signal(barrier, inc=1, device_id=(span, m), device_id_type=MESH)

    loads = [
        pltpu.make_async_copy(
            lat_hbm.at[:, :, pl.ds(g * LANES, LANES)],
            pack.at[:, pl.ds(g * wide, wide), :],
            in_sems.at[g],
        )
        for g in range(groups)
    ]
    rot_load = pltpu.make_async_copy(rot_hbm, rot, in_sems.at[groups])
    others = [
        pltpu.make_async_copy(a, b, in_sems.at[groups + 1 + i])
        for i, (a, b) in enumerate(((gain_hbm, gain), (wk_hbm, wk), (wv_hbm, wv)))
    ]
    rot_load.start()
    for d in loads + others:
        d.start()
    rot_load.wait()
    for d in loads:
        d.wait()
    half = wide // 2
    pack[:, groups * wide :, :] = jnp.concatenate([rot[:, :half, :], rot[:, half:, :]], axis=-1)
    for d in others:
        d.wait()
    wkt[...] = wk[...].T

    pl.semaphore_wait(barrier, 18)

    def send(src, dst, send_sem, recv_sem, s, m):
        return pltpu.make_async_remote_copy(
            src_ref=src, dst_ref=dst, send_sem=send_sem, recv_sem=recv_sem,
            device_id=(s, m), device_id_type=MESH,
        )

    own = pltpu.make_async_copy(pack.at[span], rows.at[model, 0], own_sem)

    def hand_on(src, m, k, zs, up_sem, down_sem, core_sem):
        dst = rows.at[m, k]
        if up_sem is not None:
            send(src, dst, z_send.at[zs], up_sem, span, up).start()
        if down_sem is not None:
            send(src, dst, z_send.at[zs], down_sem, span, down).start()
        if core_sem is not None:
            send(src, dst, c_send, core_sem, span, other).start()

    hand_on(pack.at[span], model, 0, 0, p_recv.at[0], m_recv.at[0], cown_recv.at[0])
    own.start()
    for k in range(1, 16):
        to = span ^ k
        send(pack.at[to], rows.at[model, k], a_send, a_recv.at[k], to, model).start()
    own.wait()

    @pl.loop(1, 16)
    def _(k):
        block = rows.at[model, k]
        send(block, block, a_send, a_recv.at[k], span, model).wait_recv()
        hand_on(block, model, k, 0, p_recv.at[k], m_recv.at[k], cown_recv.at[k])

    @pl.loop(0, 64 + LAG)
    def _(n):
        @pl.when(n < 64)
        def _():
            t, k = n // 16, lax.rem(n, 16)
            odd = lax.rem(k, 2)
            mp = lax.rem(model + 30 - 2 * t, 16)
            mm = lax.rem(model + 2 + 2 * t, 16)

            @pl.when((t < 3) | (odd == 0))
            def _():
                block = rows.at[mp, k]
                send(block, block, c_send, p_recv.at[n], span, up).wait_recv()

                @pl.when(t < 2)
                def _():
                    hand_on(block, mp, k, 0, p_recv.at[n + 16], None, None)

                @pl.when((t == 2) & (odd == 0))
                def _():
                    hand_on(block, mp, k, 1, p_recv.at[n + 16], None, None)

                hand_on(block, mp, k, 0, None, None, cp_recv.at[n])

            @pl.when((t < 3) | (odd == 1))
            def _():
                block = rows.at[mm, k]
                send(block, block, c_send, m_recv.at[n], span, up).wait_recv()

                @pl.when(t < 2)
                def _():
                    hand_on(block, mm, k, 0, None, m_recv.at[n + 16], None)

                @pl.when((t == 2) & (odd == 1))
                def _():
                    hand_on(block, mm, k, 1, None, m_recv.at[n + 16], None)

                hand_on(block, mm, k, 0, None, None, cm_recv.at[n])

        @pl.when(n >= LAG)
        def _():
            i = n - LAG
            t, k = i // 16, lax.rem(i, 16)
            odd = lax.rem(k, 2)
            block = rows.at[other, k]

            @pl.when(t == 0)
            def _():
                send(block, block, c_send, cown_recv.at[k], span, other).wait_recv()

            @pl.when((t < 3) | (odd == 0))
            def _():
                send(block, block, c_send, cp_recv.at[i], span, other).wait_recv()

            @pl.when((t < 3) | (odd == 1))
            def _():
                send(block, block, c_send, cm_recv.at[i], span, other).wait_recv()

            side = 1 - 2 * lax.rem(z, 2)
            shift = jnp.where(t == 0, 0, jnp.where(t == 1, 4 - side, jnp.where(t == 2, 4 + side, 2)))
            pair = lax.rem(z // 2 + shift, 4)
            blocks = [rows[4 * pair + j, k] for j in range(4)]
            keys, rotary, values = tile_of(blocks, gain, wkt, wv, groups, wide)
            at = pl.multiple_of((span ^ k) * 512 + pair * 128, 128)
            keys_ref[:128, pl.ds(at, 128)] = keys
            keys_ref[128:, pl.ds(at, 128)] = rotary
            values_ref[pl.ds(at, 128), :] = values

    send(pack.at[pl.ds(0, 15)], rows.at[model, pl.ds(0, 15)], a_send, a_recv.at[0], span, other).wait_send()
    send(rows.at[pl.ds(0, 6)], rows.at[pl.ds(0, 6)], z_send.at[0], a_recv.at[0], span, other).wait_send()
    send(rows.at[0], rows.at[0], z_send.at[1], a_recv.at[0], span, other).wait_send()
    send(rows.at[pl.ds(0, 8)], rows.at[pl.ds(0, 8)], c_send, a_recv.at[0], span, other).wait_send()


def put_out(keys_ref, values_ref, keys_hbm, values_hbm, sems):
    copies = []
    for i in range(4):
        copies.append(
            pltpu.make_async_copy(
                keys_ref.at[pl.ds(48 * i, 48)], keys_hbm.at[pl.ds(48 * i, 48)], sems.at[i]
            )
        )
        copies.append(
            pltpu.make_async_copy(
                values_ref.at[pl.ds(2048 * i, 2048)],
                values_hbm.at[pl.ds(2048 * i, 2048)],
                sems.at[4 + i],
            )
        )
    for d in copies:
        d.start()
    for d in copies:
        d.wait()


def shards(latents, rotary_rows, latent_gain, key_up, value_up):
    any_space = pl.BlockSpec(memory_space=pl.ANY)
    vmem = pl.BlockSpec(memory_space=pltpu.VMEM)
    batch, wide, depth = latents.shape
    keys_shape = jax.ShapeDtypeStruct((192, 8192), jnp.bfloat16)
    values_shape = jax.ShapeDtypeStruct((8192, 128), jnp.bfloat16)
    dma, bf16 = pltpu.SemaphoreType.DMA, jnp.bfloat16
    tall = depth // LANES * wide + wide // 2
    keys, values = pl.pallas_call(
        exchange,
        out_shape=(keys_shape, values_shape),
        in_specs=[any_space] * 5,
        out_specs=(vmem, vmem),
        scratch_shapes=[
            pltpu.VMEM((batch, tall, LANES), bf16),
            pltpu.VMEM((16, 16, tall, LANES), bf16),
            pltpu.VMEM((batch, wide, 64), bf16),
            pltpu.VMEM((1, depth), jnp.float32),
            pltpu.VMEM((depth, 128), bf16),
            pltpu.VMEM((depth, 128), bf16),
            pltpu.VMEM((128, depth), bf16),
            dma((8,)), dma, dma, dma((2,)), dma,
            dma((16,)), dma((64,)), dma((64,)), dma((16,)), dma((64,)), dma((64,)),
        ],
        compiler_params=pltpu.CompilerParams(
            collective_id=0, has_side_effects=True, vmem_limit_bytes=24 * 1024 * 1024
        ),
        cost_estimate=pl.CostEstimate(flops=2 * 8192 * 512 * 256, bytes_accessed=1 << 20, transcendentals=0),
    )(
        latents,
        rotary_rows,
        latent_gain.reshape(1, depth),
        key_up.reshape(depth, 128),
        value_up.reshape(depth, 128),
    )
    keys, values = pl.pallas_call(
        put_out,
        out_shape=(keys_shape, values_shape),
        in_specs=[vmem, vmem],
        out_specs=(any_space, any_space),
        scratch_shapes=[dma((8,))],
    )(keys, values)
    return keys.reshape(1, 1, 192, 8192), values.reshape(1, 8192, 1, 128)


def solution(mesh):
    placed = (
        P(None, ("span", "model"), None),
        P(None, ("span", "model"), None),
        P(),
        P(None, "model", None),
        P(None, "model", None),
    )
    return jax.shard_map(
        shards,
        mesh=mesh,
        in_specs=placed,
        out_specs=(P("span", "model", None, None), P("span", None, "model", None)),
        check_vma=False,
    )
```

time: 127 us -> 79.6 us (0.63)
  Pallas kernels: 0 us -> 71.3 us
  waiting for transfers between devices: 66.9 us -> 0 us
  blocking collectives: 19.2 us -> 0 us
  between operations: 14.1 us -> 0.66 us
  matrix products: 10 us -> 0 us
  other arithmetic: 6.3 us -> 0 us
  local copies, waits for them, and re-layouts: 9.92 us -> 7.4 us
    pallas_call x0 -> x2, Pallas kernels: none -> 71.3 us  [the longest x1 66.4 us: shards(): pl.pallas_call(exchange, out_shape=(keys_shape, values_shape), in_specs=[...]
    all_gather x1 -> x0, waiting for transfers between devices: 66.9 us -> none  [in_one_piece(): lax.all_gather(both, axis, axis=dim, tiled=True)]
    all_to_all x1 -> x0, blocking collectives: 19.2 us -> none  [sent_together(): lax.all_to_all(both, axis, split_axis=split_dim, concat_axis=concat_dim,...]
    dot_general x2 -> x0, matrix products: 10 us -> none  [the longest x1 6.36 us: widen_rows(): jnp.einsum('btr,rhk->bthk', rows, key_up, preferred_element_type=jnp.floa...]
    split x3 -> x0, local copies, waits for them, and re-layouts: 9.04 us -> none  [in_one_piece(): jnp.split(lax.all_gather(both, axis, axis=dim, tiled=True), ends, axis=al...]
    unnamed x6 -> x14, local copies, waits for them, and re-layouts: 0.02 us -> 7.4 us
    transpose x1 -> x0, other arithmetic: 1.95 us -> none  [shards(): decode_keys = jnp.transpose(decode_keys, (0, 2, 3, 1))]
    concatenate x2 -> x0, other arithmetic: 1.88 us -> none  [the longest x1 0.97 us: sent_together(): both = jnp.concatenate(arrays, axis=along)]
  transfers between devices with their start and end apart: 1 -> 0, of which waited for: 1 -> 0; matrix products, arithmetic and copies ran while one was open for 0% -> 0% of each run, Pallas kernels for 0% -> 0%
where the time goes in v1:
time: 79.6 us; the launch traced here: 79.4 us
  Pallas kernels  71.3 us (90%)
  local copies, waits for them, and re-layouts  7.4 us (9%)
    pallas_call x1, Pallas kernels, shards(): pl.pallas_call(exchange, out_shape=(keys_shape, values_shape), in_specs=[...  66.4 us
    unnamed x14, local copies, waits for them, and re-layouts  7.4 us
    pallas_call x1, Pallas kernels, shards(): pl.pallas_call(put_out, out_shape=(keys_shape, values_shape), in_specs=[v...  4.96 us

profile of v1, /device:TPU:1, one launch (start us, length us, event | category | flops | bytes accessed | tf_op | source)
XLA Modules:
  0.0 79.4 jit_solution(14485064807944448973)
XLA Ops:
  0.6 0.0 copy-start.2
  0.6 1.0 %copy-done.2 = bf16[16,32,512]{2,1,0:T(8,128)(2,1)S(1)} copy-done((bf16[16,32,512]{2,1,0:T(8,128)(2,1)S(1)}, bf16[16,32,512]{2,1,0:T(8,128)(2,1)}, u32[]{:S(2)}) %copy-start.2) | copy-done | bytes 524312
  1.7 0.0 copy-start.3
  1.7 0.9 %copy-done.3 = bf16[16,32,64]{2,1,0:T(8,128)(2,1)S(1)} copy-done((bf16[16,32,64]{2,1,0:T(8,128)(2,1)S(1)}, bf16[16,32,64]{2,1,0:T(8,128)(2,1)}, u32[]{:S(2)}) %copy-start.3) | copy-done | bytes 65560
  2.6 0.0 copy-start.4
  2.6 0.9 %copy-done.4 = bf16[512,1,128]{2,0,1:T(8,128)(2,1)S(1)} copy-done((bf16[512,1,128]{2,0,1:T(8,128)(2,1)S(1)}, bf16[512,1,128]{2,0,1:T(8,128)(2,1)}, u32[]{:S(2)}) %copy-start.4) | copy-done | bytes 131096
  3.5 0.0 copy-start.5
  3.5 0.9 %copy-done.5 = bf16[512,1,128]{2,0,1:T(8,128)(2,1)S(1)} copy-done((bf16[512,1,128]{2,0,1:T(8,128)(2,1)S(1)}, bf16[512,1,128]{2,0,1:T(8,128)(2,1)}, u32[]{:S(2)}) %copy-start.5) | copy-done | bytes 131096
  4.4 0.0 copy-start.6
  4.4 0.7 copy-done.6
  5.1 66.4 %shard_map.68 = (bf16[192,8192]{1,0:T(8,128)(2,1)S(1)}, bf16[8192,128]{1,0:T(8,128)(2,1)S(1)}) custom-call(bf16[16,32,512]{2,1,0:T(8,128)(2,1)S(1)} %copy-done.2, bf16[16,32,64]{2,1,0:T(8,128)(2,1)S(1)} %copy-done.3, f32[1,512]{1,0:T(1,128)S(1)} %bitcast.7, bf16[512,128]{1,0:T(8,128)(2,1)S(1)} %bitcast.5, bf16[512,128]{1,0:T(8,128)(2,1)S(1)} %bitcast.6), custom_call_target="tpu_custom_call" | custom-call | flops 2147483648 | bytes 1048576 | tf_op jit(solution)/shard_map/pallas_call | solution.py:230
  71.4 0.0 copy-start
  71.4 1.6 %copy-done = bf16[192,8192]{1,0:T(8,128)(2,1)} copy-done((bf16[192,8192]{1,0:T(8,128)(2,1)}, bf16[192,8192]{1,0:T(8,128)(2,1)S(1)}, u32[]{:S(2)}) %copy-start) | copy-done | bytes 3145752
  73.1 0.0 copy-start.1
  73.1 1.3 %copy-done.1 = bf16[8192,128]{1,0:T(8,128)(2,1)} copy-done((bf16[8192,128]{1,0:T(8,128)(2,1)}, bf16[8192,128]{1,0:T(8,128)(2,1)S(1)}, u32[]{:S(2)}) %copy-start.1) | copy-done | bytes 2097176
  74.4 5.0 %shard_map.69 = (bf16[192,8192]{1,0:T(8,128)(2,1)}, bf16[8192,128]{1,0:T(8,128)(2,1)}) custom-call(bf16[192,8192]{1,0:T(8,128)(2,1)} %copy-done, bf16[8192,128]{1,0:T(8,128)(2,1)} %copy-done.1), custom_call_target="tpu_custom_call" | custom-call | tf_op jit(solution)/shard_map/pallas_call | solution.py:257
Async XLA Ops:
  0.6 1.0 %copy-start.2 = (bf16[16,32,512]{2,1,0:T(8,128)(2,1)S(1)}, bf16[16,32,512]{2,1,0:T(8,128)(2,1)}, u32[]{:S(2)}) copy-start(bf16[16,32,512]{2,1,0:T(8,128)(2,1)} %lat_hbm.1) | copy-start | bytes 1572868
  1.7 0.9 %copy-start.3 = (bf16[16,32,64]{2,1,0:T(8,128)(2,1)S(1)}, bf16[16,32,64]{2,1,0:T(8,128)(2,1)}, u32[]{:S(2)}) copy-start(bf16[16,32,64]{2,1,0:T(8,128)(2,1)} %rot_hbm.1) | copy-start | bytes 196612
  2.6 0.9 %copy-start.4 = (bf16[512,1,128]{2,0,1:T(8,128)(2,1)S(1)}, bf16[512,1,128]{2,0,1:T(8,128)(2,1)}, u32[]{:S(2)}) copy-start(bf16[512,1,128]{2,0,1:T(8,128)(2,1)} %param.8) | copy-start | bytes 393220
  3.5 0.9 %copy-start.5 = (bf16[512,1,128]{2,0,1:T(8,128)(2,1)S(1)}, bf16[512,1,128]{2,0,1:T(8,128)(2,1)}, u32[]{:S(2)}) copy-start(bf16[512,1,128]{2,0,1:T(8,128)(2,1)} %param.9) | copy-start | bytes 393220
  4.4 0.7 copy-start.6
  71.4 1.6 %copy-start = (bf16[192,8192]{1,0:T(8,128)(2,1)}, bf16[192,8192]{1,0:T(8,128)(2,1)S(1)}, u32[]{:S(2)}) copy-start(bf16[192,8192]{1,0:T(8,128)(2,1)S(1)} %get-tuple-element.6.keys_ref) | copy-start | bytes 9437188
  73.1 1.3 %copy-start.1 = (bf16[8192,128]{1,0:T(8,128)(2,1)}, bf16[8192,128]{1,0:T(8,128)(2,1)S(1)}, u32[]{:S(2)}) copy-start(bf16[8192,128]{1,0:T(8,128)(2,1)S(1)} %get-tuple-element.7.values_ref) | copy-start | bytes 6291460

commit v2 on v0

v2 whole, which is shorter than its diff:
```python
import functools

import jax
import jax.numpy as jnp
from jax import lax
from jax.experimental import pallas as pl
from jax.experimental.pallas import tpu as pltpu
from jax.sharding import PartitionSpec as P

MESH = pl.DeviceIdType.MESH
LANES = 128
WIDE = 32
GROUPS = 4
DEPTH = GROUPS * LANES
TALL = GROUPS * WIDE + WIDE // 2
MASKS = (0, 1, 3, 4, 12, 5, 7, 13, 6, 14, 2, 15, 8, 9, 10, 11)
ARRIVALS = ((1,), (2, 3), (4, 5, 6, 7), (8, 9, 10, 11), (12, 13, 14, 15))


def normalized(rows, pair, slot, gain, xn, at):
    blocks = [rows[4 * pair + b, slot] for b in range(4)]
    x = [
        jnp.concatenate([b[g * WIDE : (g + 1) * WIDE] for b in blocks], axis=0).astype(jnp.float32)
        for g in range(GROUPS)
    ]
    squares = functools.reduce(lambda a, b: a + b, [v * v for v in x])
    scale = lax.rsqrt(jnp.sum(squares, axis=-1, keepdims=True) / DEPTH + 1e-06)
    for g in range(GROUPS):
        lanes = slice(g * LANES, (g + 1) * LANES)
        xn[at : at + LANES, lanes] = (x[g] * scale * gain[:, lanes]).astype(jnp.bfloat16)
    turned = []
    for b in blocks:
        packed = b[GROUPS * WIDE :].astype(jnp.float32)
        turned += [packed, pltpu.roll(packed, LANES // 2, 1)]
    return jnp.concatenate(turned, axis=0).astype(jnp.bfloat16)


def expand(rows, pair, slots, places, gain, w, xn, keys, values):
    rotary = [normalized(rows, pair, s, gain, xn, LANES * i) for i, s in enumerate(slots)]
    both = jnp.dot(xn[...], w[...], preferred_element_type=jnp.float32).astype(jnp.bfloat16)
    for i, at in enumerate(places):
        part = both[LANES * i : LANES * (i + 1)]
        values[pl.ds(at, LANES), :] = part[:, LANES:]
        keys[:LANES, pl.ds(at, LANES)] = part[:, :LANES].T
        keys[LANES:, pl.ds(at, LANES)] = rotary[i].T[: LANES // 2]


def place_of(source, pair):
    return pl.multiple_of(source * 512 + pair * LANES, LANES)


def mask_of(group, i):
    a, b, c, d = (MASKS[4 * g + i] for g in range(4))
    return jnp.where(group == 0, a, jnp.where(group == 1, b, jnp.where(group == 2, c, d)))


def exchange(
    lat_hbm, rot_hbm, gain_hbm, wk_hbm, wv_hbm,
    rows, keys, values, w, gain,
    pack, rot, xn,
    in_sems, a_send, z_send, c_send, a_recv, p_recv, m_recv, c_recv,
):
    span, model = lax.axis_index("span"), lax.axis_index("model")
    z, c = model // 2, lax.rem(model, 2)
    up = lax.rem(model + 2, 16)
    down = lax.rem(model + 14, 16)
    other = model + 1 - 2 * c

    barrier = pltpu.get_barrier_semaphore()
    for mask in MASKS[1:]:
        pl.semaphore_signal(barrier, inc=1, device_id=(span ^ mask, model), device_id_type=MESH)
    for m in (up, down, other):
        pl.semaphore_signal(barrier, inc=1, device_id=(span, m), device_id_type=MESH)

    pltpu.make_async_copy(rot_hbm, rot, in_sems.at[0]).start()
    for g in range(GROUPS):
        pltpu.make_async_copy(
            lat_hbm.at[:, :, pl.ds(g * LANES, LANES)],
            pack.at[:, pl.ds(g * WIDE, WIDE), :],
            in_sems.at[1],
        ).start()
    pltpu.make_async_copy(gain_hbm, gain, in_sems.at[2]).start()
    pltpu.make_async_copy(wk_hbm, w.at[:, pl.ds(0, LANES)], in_sems.at[3]).start()
    pltpu.make_async_copy(wv_hbm, w.at[:, pl.ds(LANES, LANES)], in_sems.at[3]).start()
    pltpu.make_async_copy(rot_hbm, rot, in_sems.at[0]).wait()
    half = WIDE // 2
    pack[:, GROUPS * WIDE :, :] = jnp.concatenate([rot[:, :half, :], rot[:, half:, :]], axis=-1)
    landed = pack.at[:, pl.ds(0, GROUPS * WIDE), :]
    pltpu.make_async_copy(landed, landed, in_sems.at[1]).wait()
    pl.semaphore_wait(barrier, 18)

    def send(src, dst, send_sem, recv_sem, s, m):
        return pltpu.make_async_remote_copy(
            src_ref=src, dst_ref=dst, send_sem=send_sem, recv_sem=recv_sem,
            device_id=(s, m), device_id_type=MESH,
        )

    def arrived(count, sem):
        piece = rows.at[0, pl.ds(0, count)]
        send(piece, piece, c_send, sem, span, other).wait_recv()

    def upward(src, dst, zs, sem):
        send(src, dst, z_send.at[zs], sem, span, up).start()

    def downward(src, dst, zs, sem):
        send(src, dst, z_send.at[zs], sem, span, down).start()

    def across(src, dst, sem):
        send(src, dst, c_send, sem, span, other).start()

    first, first_at = pack.at[span], rows.at[model, 0]
    upward(first, first_at, 0, p_recv.at[0])
    downward(first, first_at, 0, m_recv.at[0])
    for group, slots in enumerate(ARRIVALS):
        for slot in slots:
            to = span ^ MASKS[slot]
            send(pack.at[to], rows.at[model, slot], a_send, a_recv.at[group], to, model).start()
    across(first, first_at, c_recv.at[0])
    rows[model, 0] = pack[span]
    pltpu.make_async_copy(gain_hbm, gain, in_sems.at[2]).wait()
    pltpu.make_async_copy(w, w, in_sems.at[3]).wait()

    for group, slots in enumerate(ARRIVALS):
        arrived(len(slots), a_recv.at[group])
        piece, j = rows.at[model, pl.ds(slots[0], len(slots))], slots[0] // 4
        upward(piece, piece, 0, p_recv.at[j])
        downward(piece, piece, 0, m_recv.at[j])
        across(piece, piece, c_recv.at[j])

    side = 1 - 2 * lax.rem(z, 2)

    @pl.loop(0, 17)
    def _(n):
        @pl.when(n < 16)
        def _():
            t, j = n // 4, lax.rem(n, 4)
            mp = lax.rem(model + 30 - 2 * t, 16)
            mm = lax.rem(model + 2 + 2 * t, 16)
            from_below, from_above = rows.at[mp, pl.ds(4 * j, 4)], rows.at[mm, pl.ds(4 * j, 4)]
            low, high = rows.at[mp, pl.ds(4 * j, 2)], rows.at[mm, pl.ds(4 * j + 2, 2)]

            @pl.when(t < 3)
            def _():
                arrived(4, p_recv.at[n])

                @pl.when(t < 2)
                def _():
                    upward(from_below, from_below, 0, p_recv.at[n + 4])

                @pl.when(t == 2)
                def _():
                    upward(low, low, 1, p_recv.at[n + 4])

                arrived(4, m_recv.at[n])

                @pl.when(t < 2)
                def _():
                    downward(from_above, from_above, 0, m_recv.at[n + 4])

                @pl.when(t == 2)
                def _():
                    downward(high, high, 1, m_recv.at[n + 4])

                across(from_below, from_below, c_recv.at[n])
                across(from_above, from_above, c_recv.at[n])

            @pl.when(t == 3)
            def _():
                arrived(2, p_recv.at[n])
                across(low, low, c_recv.at[n])
                arrived(2, m_recv.at[n])
                across(high, high, c_recv.at[n])

        @pl.when(n >= 1)
        def _():
            i = n - 1
            t, j = i // 4, lax.rem(i, 4)

            @pl.when(t == 0)
            def _():
                arrived(12, c_recv.at[i])

            @pl.when((t == 1) | (t == 2))
            def _():
                arrived(8, c_recv.at[i])

            @pl.when(t == 3)
            def _():
                arrived(4, c_recv.at[i])

            @pl.when(i < 15)
            def _():
                shift = jnp.where(
                    t == 0, 0, jnp.where(t == 1, 4 - side, jnp.where(t == 2, 4 + side, 2))
                )
                pair = lax.rem(z // 2 + shift, 4)
                expand(
                    rows, pair, [4 * j + s for s in range(4)],
                    [place_of(span ^ mask_of(j, s), pair) for s in range(4)],
                    gain, w, xn, keys, values,
                )

    send(pack.at[pl.ds(0, 15)], rows.at[0, pl.ds(0, 15)], a_send, a_recv.at[0], span, other).wait_send()
    send(rows.at[pl.ds(0, 6)], rows.at[pl.ds(0, 6)], z_send.at[0], a_recv.at[0], span, other).wait_send()
    send(rows.at[0], rows.at[0], z_send.at[1], a_recv.at[0], span, other).wait_send()
    send(rows.at[pl.ds(0, 8)], rows.at[pl.ds(0, 8)], c_send, a_recv.at[0], span, other).wait_send()


def finish(rows, keys, values, w, gain, keys_hbm, values_hbm, xn, last_keys, last_values, sems):
    span, model = lax.axis_index("span"), lax.axis_index("model")
    last = (span // 4) ^ 2
    pair = lax.rem(model // 4 + 2, 4)
    places = [place_of(span ^ mask, pair) for mask in MASKS[12:]]

    def leave(keys_from, k, values_from, v):
        pltpu.make_async_copy(keys_from, keys_hbm.at[:, k], sems.at[0]).start()
        pltpu.make_async_copy(values_from, values_hbm.at[v], sems.at[1]).start()

    for i in range(1, 4):
        at = pl.ds(pl.multiple_of((last ^ i) * 2048, 2048), 2048)
        leave(keys.at[:, at], at, values.at[at], at)
    for i in range(4):
        for other in range(1, 4):
            at = pl.ds(place_of(last * 4 + i, lax.rem(pair + other, 4)), LANES)
            leave(keys.at[:, at], at, values.at[at], at)
    expand(
        rows, pair, range(12, 16), [LANES * i for i in range(4)], gain, w, xn, last_keys, last_values
    )
    for i in range(4):
        here, at = pl.ds(LANES * i, LANES), pl.ds(places[i], LANES)
        leave(last_keys.at[:, here], at, last_values.at[here], at)
    pltpu.make_async_copy(keys, keys_hbm, sems.at[0]).wait()
    pltpu.make_async_copy(values, values_hbm, sems.at[1]).wait()


def shards(latents, rotary_rows, latent_gain, key_up, value_up):
    hbm = pl.BlockSpec(memory_space=pltpu.HBM)
    vmem = pl.BlockSpec(memory_space=pltpu.VMEM)
    dma, bf16, f32 = pltpu.SemaphoreType.DMA, jnp.bfloat16, jnp.float32
    keys_shape = jax.ShapeDtypeStruct((192, 8192), bf16)
    values_shape = jax.ShapeDtypeStruct((8192, 128), bf16)
    ready = pl.pallas_call(
        exchange,
        out_shape=(
            jax.ShapeDtypeStruct((16, 16, TALL, LANES), bf16),
            keys_shape,
            values_shape,
            jax.ShapeDtypeStruct((DEPTH, 2 * LANES), bf16),
            jax.ShapeDtypeStruct((1, DEPTH), f32),
        ),
        in_specs=[hbm] * 5,
        out_specs=(vmem,) * 5,
        scratch_shapes=[
            pltpu.VMEM((16, TALL, LANES), bf16),
            pltpu.VMEM((16, WIDE, 64), bf16),
            pltpu.VMEM((512, DEPTH), bf16),
            dma((4,)), dma, dma((2,)), dma,
            dma((5,)), dma((16,)), dma((16,)), dma((16,)),
        ],
        compiler_params=pltpu.CompilerParams(
            collective_id=0, has_side_effects=True, vmem_limit_bytes=8 * 1024 * 1024
        ),
        cost_estimate=pl.CostEstimate(flops=2 * 8192 * 512 * 256, bytes_accessed=1 << 20, transcendentals=0),
    )(
        *(
            pltpu.with_memory_space_constraint(a, pltpu.HBM)
            for a in (
                latents,
                rotary_rows,
                latent_gain.reshape(1, DEPTH),
                key_up.reshape(DEPTH, LANES),
                value_up.reshape(DEPTH, LANES),
            )
        )
    )
    keys, values = pl.pallas_call(
        finish,
        out_shape=(keys_shape, values_shape),
        in_specs=[vmem] * 5,
        out_specs=(hbm, hbm),
        scratch_shapes=[
            pltpu.VMEM((512, DEPTH), bf16),
            pltpu.VMEM((192, 512), bf16),
            pltpu.VMEM((512, LANES), bf16),
            dma((2,)),
        ],
        compiler_params=pltpu.CompilerParams(vmem_limit_bytes=4 * 1024 * 1024),
    )(*ready)
    return keys.reshape(1, 1, 192, 8192), values.reshape(1, 8192, 1, 128)


def solution(mesh):
    placed = (
        P(None, ("span", "model"), None),
        P(None, ("span", "model"), None),
        P(),
        P(None, "model", None),
        P(None, "model", None),
    )
    return jax.shard_map(
        shards,
        mesh=mesh,
        in_specs=placed,
        out_specs=(P("span", "model", None, None), P("span", None, "model", None)),
        check_vma=False,
    )
```

time: 127 us -> 64 us (0.50)
  waiting for transfers between devices: 66.9 us -> 0 us
  Pallas kernels: 0 us -> 63.3 us
  blocking collectives: 19.2 us -> 0 us
  between operations: 14.1 us -> 0.64 us
  matrix products: 10 us -> 0 us
  local copies, waits for them, and re-layouts: 9.92 us -> 0 us
  other arithmetic: 6.3 us -> 0 us
    all_gather x1 -> x0, waiting for transfers between devices: 66.9 us -> none  [in_one_piece(): lax.all_gather(both, axis, axis=dim, tiled=True)]
    pallas_call x0 -> x2, Pallas kernels: none -> 63.3 us  [the longest x1 60.7 us: shards(): pl.pallas_call(exchange, out_shape=(jax.ShapeDtypeStruct((16, 16, TALL, L...]
    all_to_all x1 -> x0, blocking collectives: 19.2 us -> none  [sent_together(): lax.all_to_all(both, axis, split_axis=split_dim, concat_axis=concat_dim,...]
    dot_general x2 -> x0, matrix products: 10 us -> none  [the longest x1 6.36 us: widen_rows(): jnp.einsum('btr,rhk->bthk', rows, key_up, preferred_element_type=jnp.floa...]
    split x3 -> x0, local copies, waits for them, and re-layouts: 9.04 us -> none  [in_one_piece(): jnp.split(lax.all_gather(both, axis, axis=dim, tiled=True), ends, axis=al...]
    transpose x1 -> x0, other arithmetic: 1.95 us -> none  [shards(): decode_keys = jnp.transpose(decode_keys, (0, 2, 3, 1))]
    concatenate x2 -> x0, other arithmetic: 1.88 us -> none  [the longest x1 0.97 us: sent_together(): both = jnp.concatenate(arrays, axis=along)]
  transfers between devices with their start and end apart: 1 -> 0, of which waited for: 1 -> 0; matrix products, arithmetic and copies ran while one was open for 0% -> 0% of each run, Pallas kernels for 0% -> 0%
where the time goes in v2:
time: 64 us; the launch traced here: 63.9 us
  Pallas kernels  63.3 us (99%)
  between operations  0.64 us (1%)
    pallas_call x1, Pallas kernels, shards(): pl.pallas_call(exchange, out_shape=(jax.ShapeDtypeStruct((16, 16, TALL, L...  60.7 us
    pallas_call x1, Pallas kernels, shards(): pl.pallas_call(finish, out_shape=(keys_shape, values_shape), in_specs=[vm...  2.61 us

profile of v2, /device:TPU:1, one launch (start us, length us, event | category | flops | bytes accessed | tf_op | source)
XLA Modules:
  0.0 63.9 jit_solution(948667338530298398)
XLA Ops:
  0.6 60.7 %shard_map.68 = (bf16[16,16,144,128]{3,2,1,0:T(8,128)(2,1)S(1)}, bf16[192,8192]{1,0:T(8,128)(2,1)S(1)}, bf16[8192,128]{1,0:T(8,128)(2,1)S(1)}, bf16[512,256]{1,0:T(8,128)(2,1)S(1)}, f32[1,512]{1,0:T(1,128)S(1)}) custom-call(bf16[16,32,512]{2,1,0:T(8,128)(2,1)} %lat_hbm.1, bf16[16,32,64]{2,1,0:T(8,128)(2,1)} %rot_hbm.1, f32[1,512]{1,0:T(1,128)} %bitcast.9, ...), custom_call_target="tpu_custom_call" | custom-call | flops 2147483648 | bytes 1048576 | tf_op jit(solution)/shard_map/pallas_call | solution.py:242
  61.3 2.6 %shard_map.69 = (bf16[192,8192]{1,0:T(8,128)(2,1)}, bf16[8192,128]{1,0:T(8,128)(2,1)}) custom-call(bf16[16,16,144,128]{3,2,1,0:T(8,128)(2,1)S(1)} %get-tuple-element.9.rows, bf16[192,8192]{1,0:T(8,128)(2,1)S(1)} %get-tuple-element.10.keys, bf16[8192,128]{1,0:T(8,128)(2,1)S(1)} %get-tuple-element.11.values, bf16[512,256]{1,0:T(8,128)(2,1)S(1)} %get-tuple-element.12.w, ...), custom_call_target="tpu_custom_call" | custom-call | tf_op jit(solution)/shard_map/pallas_call | solution.py:276

commit v3 on v2

--- a/solution.py
+++ b/solution.py
@@ -13,8 +13,13 @@
 GROUPS = 4
 DEPTH = GROUPS * LANES
 TALL = GROUPS * WIDE + WIDE // 2
-MASKS = (0, 1, 3, 4, 12, 5, 7, 13, 6, 14, 2, 15, 8, 9, 10, 11)
-ARRIVALS = ((1,), (2, 3), (4, 5, 6, 7), (8, 9, 10, 11), (12, 13, 14, 15))
+MASKS = (0, 1, 3, 4, 12, 5, 7, 13, 2, 15, 6, 14, 8, 9, 10, 11)
+NEAR, MIDDLE, FAR = (1, 2, 3, 4), (5, 6, 7), (8, 9, 12, 10, 11, 13, 15, 14)
+RISING = (2, 2, 1, 1)
+
+
+def hops(mask):
+    return (0, 1, 2, 1)[mask % 4] + (0, 1, 2, 1)[mask // 4]
 
 
 def normalized(rows, pair, slot, gain, xn, at):
@@ -57,8 +62,8 @@
 def exchange(
     lat_hbm, rot_hbm, gain_hbm, wk_hbm, wv_hbm,
     rows, keys, values, w, gain,
-    pack, rot, xn,
-    in_sems, a_send, z_send, c_send, a_recv, p_recv, m_recv, c_recv,
+    pack, rot, xn, stage_up, stage_down,
+    in_sems, a_send, r_send, z_send, c_send, a_recv, p_recv, m_recv, c_recv, stage_recv, token,
 ):
     span, model = lax.axis_index("span"), lax.axis_index("model")
     z, c = model // 2, lax.rem(model, 2)
@@ -67,10 +72,11 @@
     other = model + 1 - 2 * c
 
     barrier = pltpu.get_barrier_semaphore()
-    for mask in MASKS[1:]:
-        pl.semaphore_signal(barrier, inc=1, device_id=(span ^ mask, model), device_id_type=MESH)
     for m in (up, down, other):
         pl.semaphore_signal(barrier, inc=1, device_id=(span, m), device_id_type=MESH)
+    near = [span ^ MASKS[slot] for slot in NEAR]
+    for s in near:
+        pl.semaphore_signal(barrier, inc=1, device_id=(s, model), device_id_type=MESH)
 
     pltpu.make_async_copy(rot_hbm, rot, in_sems.at[0]).start()
     for g in range(GROUPS):
@@ -87,7 +93,7 @@
     pack[:, GROUPS * WIDE :, :] = jnp.concatenate([rot[:, :half, :], rot[:, half:, :]], axis=-1)
     landed = pack.at[:, pl.ds(0, GROUPS * WIDE), :]
     pltpu.make_async_copy(landed, landed, in_sems.at[1]).wait()
-    pl.semaphore_wait(barrier, 18)
+    pl.semaphore_wait(barrier, 7)
 
     def send(src, dst, send_sem, recv_sem, s, m):
         return pltpu.make_async_remote_copy(
@@ -108,99 +114,140 @@
     def across(src, dst, sem):
         send(src, dst, c_send, sem, span, other).start()
 
+    def spread(slot, sem):
+        to = span ^ MASKS[slot]
+        send(pack.at[to], rows.at[model, slot], a_send, a_recv.at[sem], to, model).start()
+
     first, first_at = pack.at[span], rows.at[model, 0]
     upward(first, first_at, 0, p_recv.at[0])
     downward(first, first_at, 0, m_recv.at[0])
-    for group, slots in enumerate(ARRIVALS):
+    for slot in NEAR + MIDDLE:
+        src, sem = pack.at[span ^ MASKS[slot]], slot // 5
+        upward(src, stage_up.at[slot - 1], 0, stage_recv.at[sem])
+        downward(src, stage_down.at[slot - 1], 0, stage_recv.at[2 + sem])
+    for slot in NEAR:
+        spread(slot, 0)
+
+    for far in range(2, 5):
+        for s in near:
+            pl.semaphore_signal(token.at[far - 2], inc=1, device_id=(s, model), device_id_type=MESH)
+        if far == 2:
+            across(first, first_at, c_recv.at[0])
+            rows[model, 0] = pack[span]
+        pl.semaphore_wait(token.at[far - 2], 4)
+        for i, slot in enumerate(FAR):
+            if hops(MASKS[slot]) == far:
+                spread(slot, 2 + i)
+    for slot in MIDDLE:
+        spread(slot, 1)
+
+    def relay(slots, stage, sem, origin, recv):
+        piece = rows.at[origin, pl.ds(slots[0], len(slots))]
+        part = stage.at[pl.ds(slots[0] - 1, len(slots))]
+        send(part, piece, r_send, stage_recv.at[sem], span, up).wait_recv()
         for slot in slots:
-            to = span ^ MASKS[slot]
-            send(pack.at[to], rows.at[model, slot], a_send, a_recv.at[group], to, model).start()
-    across(first, first_at, c_recv.at[0])
-    rows[model, 0] = pack[span]
+            send(
+                stage.at[slot - 1], rows.at[origin, slot], r_send, recv.at[slot // 4],
+                span ^ MASKS[slot], model,
+            ).start()
+
+    for i, slot in enumerate(FAR):
+        arrived(1, a_recv.at[2 + i])
+        piece = rows.at[model, slot]
+        upward(piece, piece, 0, p_recv.at[slot // 4])
+        downward(piece, piece, 0, m_recv.at[slot // 4])
+        if i == 2:
+            relay(NEAR, stage_up, 0, down, p_recv)
+            relay(NEAR, stage_down, 2, up, m_recv)
+        if i == 6:
+            relay(MIDDLE, stage_up, 1, down, p_recv)
+            relay(MIDDLE, stage_down, 3, up, m_recv)
+    arrived(4, a_recv.at[0])
+    arrived(3, a_recv.at[1])
+    for start, count in ((1, 3), (4, 4), (8, 4), (12, 4)):
+        piece = rows.at[model, pl.ds(start, count)]
+        across(piece, piece, c_recv.at[start // 4])
     pltpu.make_async_copy(gain_hbm, gain, in_sems.at[2]).wait()
     pltpu.make_async_copy(w, w, in_sems.at[3]).wait()
 
-    for group, slots in enumerate(ARRIVALS):
-        arrived(len(slots), a_recv.at[group])
-        piece, j = rows.at[model, pl.ds(slots[0], len(slots))], slots[0] // 4
-        upward(piece, piece, 0, p_recv.at[j])
-        downward(piece, piece, 0, m_recv.at[j])
-        across(piece, piece, c_recv.at[j])
-
     side = 1 - 2 * lax.rem(z, 2)
 
-    @pl.loop(0, 17)
+    def tile(t, j):
+        shift = jnp.where(t == 0, 0, jnp.where(t == 1, 4 - side, jnp.where(t == 2, 4 + side, 2)))
+        pair = lax.rem(z // 2 + shift, 4)
+        expand(
+            rows, pair, [4 * j + s for s in range(4)],
+            [place_of(span ^ mask_of(j, s), pair) for s in range(4)],
+            gain, w, xn, keys, values,
+        )
+
+    @pl.loop(0, 12)
     def _(n):
-        @pl.when(n < 16)
+        t, j = n // 4, lax.rem(n, 4)
+        mp = lax.rem(model + 30 - 2 * t, 16)
+        mm = lax.rem(model + 2 + 2 * t, 16)
+        from_below, from_above = rows.at[mp, pl.ds(4 * j, 4)], rows.at[mm, pl.ds(4 * j, 4)]
+        arrived(4, p_recv.at[n])
+
+        @pl.when(t < 2)
         def _():
-            t, j = n // 4, lax.rem(n, 4)
-            mp = lax.rem(model + 30 - 2 * t, 16)
-            mm = lax.rem(model + 2 + 2 * t, 16)
-            from_below, from_above = rows.at[mp, pl.ds(4 * j, 4)], rows.at[mm, pl.ds(4 * j, 4)]
-            low, high = rows.at[mp, pl.ds(4 * j, 2)], rows.at[mm, pl.ds(4 * j + 2, 2)]
-
-            @pl.when(t < 3)
+            upward(from_below, from_below, 0, p_recv.at[n + 4])
+
+        for part, count in enumerate(RISING):
+
+            @pl.when(n == 8 + part)
             def _():
-                arrived(4, p_recv.at[n])
-
-                @pl.when(t < 2)
-                def _():
-                    upward(from_below, from_below, 0, p_recv.at[n + 4])
-
-                @pl.when(t == 2)
-                def _():
-                    upward(low, low, 1, p_recv.at[n + 4])
-
-                arrived(4, m_recv.at[n])
-
-                @pl.when(t < 2)
-                def _():
-                    downward(from_above, from_above, 0, m_recv.at[n + 4])
-
-                @pl.when(t == 2)
-                def _():
-                    downward(high, high, 1, m_recv.at[n + 4])
-
-                across(from_below, from_below, c_recv.at[n])
-                across(from_above, from_above, c_recv.at[n])
-
-            @pl.when(t == 3)
+                piece = rows.at[mp, pl.ds(4 * part, count)]
+                upward(piece, piece, 1, p_recv.at[12 + part])
+
+        arrived(4, m_recv.at[n])
+
+        @pl.when(t < 2)
+        def _():
+            downward(from_above, from_above, 0, m_recv.at[n + 4])
+
+        for part, count in enumerate(RISING):
+
+            @pl.when(n == 8 + part)
             def _():
-                arrived(2, p_recv.at[n])
-                across(low, low, c_recv.at[n])
-                arrived(2, m_recv.at[n])
-                across(high, high, c_recv.at[n])
+                piece = rows.at[mm, pl.ds(4 * part + count, 4 - count)]
+                downward(piece, piece, 1, m_recv.at[12 + part])
+
+        across(from_below, from_below, c_recv.at[n])
+        across(from_above, from_above, c_recv.at[n])
 
         @pl.when(n >= 1)
         def _():
             i = n - 1
-            t, j = i // 4, lax.rem(i, 4)
-
-            @pl.when(t == 0)
+
+            @pl.when(i < 4)
             def _():
                 arrived(12, c_recv.at[i])
 
-            @pl.when((t == 1) | (t == 2))
+            @pl.when(i >= 4)
             def _():
                 arrived(8, c_recv.at[i])
 
-            @pl.when(t == 3)
-            def _():
-                arrived(4, c_recv.at[i])
-
-            @pl.when(i < 15)
-            def _():
-                shift = jnp.where(
-                    t == 0, 0, jnp.where(t == 1, 4 - side, jnp.where(t == 2, 4 + side, 2))
-                )
-                pair = lax.rem(z // 2 + shift, 4)
-                expand(
-                    rows, pair, [4 * j + s for s in range(4)],
-                    [place_of(span ^ mask_of(j, s), pair) for s in range(4)],
-                    gain, w, xn, keys, values,
-                )
+            tile(i // 4, lax.rem(i, 4))
+
+    opposite = lax.rem(model + 8, 16)
+    for part, count in enumerate(RISING):
+        low = rows.at[opposite, pl.ds(4 * part, count)]
+        high = rows.at[opposite, pl.ds(4 * part + count, 4 - count)]
+        arrived(count, p_recv.at[12 + part])
+        across(low, low, c_recv.at[12 + part])
+        arrived(4 - count, m_recv.at[12 + part])
+        across(high, high, c_recv.at[12 + part])
+        if part == 0:
+            arrived(8, c_recv.at[11])
+            tile(2, 3)
+        else:
+            arrived(4, c_recv.at[11 + part])
+            tile(3, part - 1)
+    arrived(4, c_recv.at[15])
 
     send(pack.at[pl.ds(0, 15)], rows.at[0, pl.ds(0, 15)], a_send, a_recv.at[0], span, other).wait_send()
+    send(rows.at[0, pl.ds(0, 14)], rows.at[0, pl.ds(0, 14)], r_send, a_recv.at[0], span, other).wait_send()
     send(rows.at[pl.ds(0, 6)], rows.at[pl.ds(0, 6)], z_send.at[0], a_recv.at[0], span, other).wait_send()
     send(rows.at[0], rows.at[0], z_send.at[1], a_recv.at[0], span, other).wait_send()
     send(rows.at[pl.ds(0, 8)], rows.at[pl.ds(0, 8)], c_send, a_recv.at[0], span, other).wait_send()
@@ -254,8 +301,11 @@
             pltpu.VMEM((16, TALL, LANES), bf16),
             pltpu.VMEM((16, WIDE, 64), bf16),
             pltpu.VMEM((512, DEPTH), bf16),
-            dma((4,)), dma, dma((2,)), dma,
-            dma((5,)), dma((16,)), dma((16,)), dma((16,)),
+            pltpu.VMEM((7, TALL, LANES), bf16),
+            pltpu.VMEM((7, TALL, LANES), bf16),
+            dma((4,)), dma, dma, dma((2,)), dma,
+            dma((10,)), dma((16,)), dma((16,)), dma((16,)), dma((4,)),
+            pltpu.SemaphoreType.REGULAR((3,)),
         ],
         compiler_params=pltpu.CompilerParams(
             collective_id=0, has_side_effects=True, vmem_limit_bytes=8 * 1024 * 1024

time: 64 us -> 61.7 us (0.964)
  Pallas kernels: 63.3 us -> 61 us
    pallas_call x1, Pallas kernels: 60.7 us -> 58.4 us  [shards(): pl.pallas_call(exchange, out_shape=(jax.ShapeDtypeStruct((16, 16, TALL, L...]
where the time goes in v3:
time: 61.7 us; the launch traced here: 61.6 us
  Pallas kernels  61 us (99%)
  between operations  0.64 us (1%)
    pallas_call x1, Pallas kernels, shards(): pl.pallas_call(exchange, out_shape=(jax.ShapeDtypeStruct((16, 16, TALL, L...  58.4 us
    pallas_call x1, Pallas kernels, shards(): pl.pallas_call(finish, out_shape=(keys_shape, values_shape), in_specs=[vm...  2.61 us

profile of v3, /device:TPU:1, one launch (start us, length us, event | category | flops | bytes accessed | tf_op | source)
XLA Modules:
  0.0 61.6 jit_solution(15985855820229119301)
XLA Ops:
  0.6 58.4 %shard_map.68 = (bf16[16,16,144,128]{3,2,1,0:T(8,128)(2,1)S(1)}, bf16[192,8192]{1,0:T(8,128)(2,1)S(1)}, bf16[8192,128]{1,0:T(8,128)(2,1)S(1)}, bf16[512,256]{1,0:T(8,128)(2,1)S(1)}, f32[1,512]{1,0:T(1,128)S(1)}) custom-call(bf16[16,32,512]{2,1,0:T(8,128)(2,1)} %lat_hbm.1, bf16[16,32,64]{2,1,0:T(8,128)(2,1)} %rot_hbm.1, f32[1,512]{1,0:T(1,128)} %bitcast.9, ...), custom_call_target="tpu_custom_call" | custom-call | flops 2147483648 | bytes 1048576 | tf_op jit(solution)/shard_map/pallas_call | solution.py:289
  59.0 2.6 %shard_map.69 = (bf16[192,8192]{1,0:T(8,128)(2,1)}, bf16[8192,128]{1,0:T(8,128)(2,1)}) custom-call(bf16[16,16,144,128]{3,2,1,0:T(8,128)(2,1)S(1)} %get-tuple-element.9.rows, bf16[192,8192]{1,0:T(8,128)(2,1)S(1)} %get-tuple-element.10.keys, bf16[8192,128]{1,0:T(8,128)(2,1)S(1)} %get-tuple-element.11.values, bf16[512,256]{1,0:T(8,128)(2,1)S(1)} %get-tuple-element.12.w, ...), custom_call_target="tpu_custom_call" | custom-call | tf_op jit(solution)/shard_map/pallas_call | solution.py:326

commit v4 on v3

--- a/solution.py
+++ b/solution.py
@@ -14,12 +14,8 @@
 DEPTH = GROUPS * LANES
 TALL = GROUPS * WIDE + WIDE // 2
 MASKS = (0, 1, 3, 4, 12, 5, 7, 13, 2, 15, 6, 14, 8, 9, 10, 11)
-NEAR, MIDDLE, FAR = (1, 2, 3, 4), (5, 6, 7), (8, 9, 12, 10, 11, 13, 15, 14)
+NEAR, MIDDLE, FAR = (1, 2, 3, 4), (5, 6, 7, 8, 9, 12), (10, 11, 13, 14, 15)
 RISING = (2, 2, 1, 1)
-
-
-def hops(mask):
-    return (0, 1, 2, 1)[mask % 4] + (0, 1, 2, 1)[mask // 4]
 
 
 def normalized(rows, pair, slot, gain, xn, at):
@@ -118,53 +114,52 @@
         to = span ^ MASKS[slot]
         send(pack.at[to], rows.at[model, slot], a_send, a_recv.at[sem], to, model).start()
 
+    def onward(slot, sem):
+        arrived(1, a_recv.at[sem])
+        piece = rows.at[model, slot]
+        upward(piece, piece, 0, p_recv.at[slot // 4])
+        downward(piece, piece, 0, m_recv.at[slot // 4])
+
+    def tell(turn):
+        for s in near:
+            pl.semaphore_signal(token.at[turn], inc=1, device_id=(s, model), device_id_type=MESH)
+
     first, first_at = pack.at[span], rows.at[model, 0]
     upward(first, first_at, 0, p_recv.at[0])
     downward(first, first_at, 0, m_recv.at[0])
-    for slot in NEAR + MIDDLE:
-        src, sem = pack.at[span ^ MASKS[slot]], slot // 5
-        upward(src, stage_up.at[slot - 1], 0, stage_recv.at[sem])
-        downward(src, stage_down.at[slot - 1], 0, stage_recv.at[2 + sem])
-    for slot in NEAR:
-        spread(slot, 0)
-
-    for far in range(2, 5):
-        for s in near:
-            pl.semaphore_signal(token.at[far - 2], inc=1, device_id=(s, model), device_id_type=MESH)
-        if far == 2:
-            across(first, first_at, c_recv.at[0])
-            rows[model, 0] = pack[span]
-        pl.semaphore_wait(token.at[far - 2], 4)
+    for i, slot in enumerate(NEAR):
+        spread(slot, i)
+    tell(0)
+    for i, slot in enumerate(FAR):
+        src = pack.at[span ^ MASKS[slot]]
+        upward(src, stage_up.at[i], 0, stage_recv.at[0])
+        downward(src, stage_down.at[i], 0, stage_recv.at[1])
+    across(first, first_at, c_recv.at[0])
+    rows[model, 0] = pack[span]
+    pl.semaphore_wait(token.at[0], 4)
+    for i, slot in enumerate(MIDDLE):
+        spread(slot, 4 + i)
+    tell(1)
+    for i, slot in enumerate(NEAR):
+        onward(slot, i)
+    pl.semaphore_wait(token.at[1], 4)
+    tell(2)
+    for i, slot in enumerate(MIDDLE[:2]):
+        onward(slot, 4 + i)
+    pl.semaphore_wait(token.at[2], 4)
+    for i, slot in enumerate(MIDDLE[2:]):
+        onward(slot, 6 + i)
+
+    for stage, sem, origin, recv in ((stage_up, 0, down, p_recv), (stage_down, 1, up, m_recv)):
+        send(stage, stage, r_send, stage_recv.at[sem], span, up).wait_recv()
         for i, slot in enumerate(FAR):
-            if hops(MASKS[slot]) == far:
-                spread(slot, 2 + i)
-    for slot in MIDDLE:
-        spread(slot, 1)
-
-    def relay(slots, stage, sem, origin, recv):
-        piece = rows.at[origin, pl.ds(slots[0], len(slots))]
-        part = stage.at[pl.ds(slots[0] - 1, len(slots))]
-        send(part, piece, r_send, stage_recv.at[sem], span, up).wait_recv()
-        for slot in slots:
             send(
-                stage.at[slot - 1], rows.at[origin, slot], r_send, recv.at[slot // 4],
+                stage.at[i], rows.at[origin, slot], r_send, recv.at[slot // 4],
                 span ^ MASKS[slot], model,
             ).start()
-
-    for i, slot in enumerate(FAR):
-        arrived(1, a_recv.at[2 + i])
-        piece = rows.at[model, slot]
-        upward(piece, piece, 0, p_recv.at[slot // 4])
-        downward(piece, piece, 0, m_recv.at[slot // 4])
-        if i == 2:
-            relay(NEAR, stage_up, 0, down, p_recv)
-            relay(NEAR, stage_down, 2, up, m_recv)
-        if i == 6:
-            relay(MIDDLE, stage_up, 1, down, p_recv)
-            relay(MIDDLE, stage_down, 3, up, m_recv)
-    arrived(4, a_recv.at[0])
-    arrived(3, a_recv.at[1])
-    for start, count in ((1, 3), (4, 4), (8, 4), (12, 4)):
+    for slot in FAR:
+        spread(slot, 10)
+    for start, count in ((1, 3), (4, 4), (8, 2), (12, 1)):
         piece = rows.at[model, pl.ds(start, count)]
         across(piece, piece, c_recv.at[start // 4])
     pltpu.make_async_copy(gain_hbm, gain, in_sems.at[2]).wait()
@@ -212,6 +207,13 @@
             def _():
                 piece = rows.at[mm, pl.ds(4 * part + count, 4 - count)]
                 downward(piece, piece, 1, m_recv.at[12 + part])
+
+        @pl.when(n == 2)
+        def _():
+            arrived(5, a_recv.at[10])
+            for start, count in ((10, 2), (13, 3)):
+                piece = rows.at[model, pl.ds(start, count)]
+                across(piece, piece, c_recv.at[start // 4])
 
         across(from_below, from_below, c_recv.at[n])
         across(from_above, from_above, c_recv.at[n])
@@ -247,7 +249,7 @@
     arrived(4, c_recv.at[15])
 
     send(pack.at[pl.ds(0, 15)], rows.at[0, pl.ds(0, 15)], a_send, a_recv.at[0], span, other).wait_send()
-    send(rows.at[0, pl.ds(0, 14)], rows.at[0, pl.ds(0, 14)], r_send, a_recv.at[0], span, other).wait_send()
+    send(rows.at[0, pl.ds(0, 10)], rows.at[0, pl.ds(0, 10)], r_send, a_recv.at[0], span, other).wait_send()
     send(rows.at[pl.ds(0, 6)], rows.at[pl.ds(0, 6)], z_send.at[0], a_recv.at[0], span, other).wait_send()
     send(rows.at[0], rows.at[0], z_send.at[1], a_recv.at[0], span, other).wait_send()
     send(rows.at[pl.ds(0, 8)], rows.at[pl.ds(0, 8)], c_send, a_recv.at[0], span, other).wait_send()
@@ -301,10 +303,10 @@
             pltpu.VMEM((16, TALL, LANES), bf16),
             pltpu.VMEM((16, WIDE, 64), bf16),
             pltpu.VMEM((512, DEPTH), bf16),
-            pltpu.VMEM((7, TALL, LANES), bf16),
-            pltpu.VMEM((7, TALL, LANES), bf16),
+            pltpu.VMEM((len(FAR), TALL, LANES), bf16),
+            pltpu.VMEM((len(FAR), TALL, LANES), bf16),
             dma((4,)), dma, dma, dma((2,)), dma,
-            dma((10,)), dma((16,)), dma((16,)), dma((16,)), dma((4,)),
+            dma((11,)), dma((16,)), dma((16,)), dma((16,)), dma((2,)),
             pltpu.SemaphoreType.REGULAR((3,)),
         ],
         compiler_params=pltpu.CompilerParams(

time: 61.7 us -> 59.3 us (0.961)
  Pallas kernels: 61 us -> 58.6 us
    pallas_call x1, Pallas kernels: 58.4 us -> 56 us  [shards(): pl.pallas_call(exchange, out_shape=(jax.ShapeDtypeStruct((16, 16, TALL, L...]
where the time goes in v4:
time: 59.3 us; the launch traced here: 59.2 us
  Pallas kernels  58.6 us (99%)
  between operations  0.64 us (1%)
    pallas_call x1, Pallas kernels, shards(): pl.pallas_call(exchange, out_shape=(jax.ShapeDtypeStruct((16, 16, TALL, L...  56 us
    pallas_call x1, Pallas kernels, shards(): pl.pallas_call(finish, out_shape=(keys_shape, values_shape), in_specs=[vm...  2.61 us

profile of v4, /device:TPU:1, one launch (start us, length us, event | category | flops | bytes accessed | tf_op | source)
XLA Modules:
  0.0 59.2 jit_solution(14601402027510395048)
XLA Ops:
  0.6 56.0 %shard_map.68 = (bf16[16,16,144,128]{3,2,1,0:T(8,128)(2,1)S(1)}, bf16[192,8192]{1,0:T(8,128)(2,1)S(1)}, bf16[8192,128]{1,0:T(8,128)(2,1)S(1)}, bf16[512,256]{1,0:T(8,128)(2,1)S(1)}, f32[1,512]{1,0:T(1,128)S(1)}) custom-call(bf16[16,32,512]{2,1,0:T(8,128)(2,1)} %lat_hbm.1, bf16[16,32,64]{2,1,0:T(8,128)(2,1)} %rot_hbm.1, f32[1,512]{1,0:T(1,128)} %bitcast.9, ...), custom_call_target="tpu_custom_call" | custom-call | flops 2147483648 | bytes 1048576 | tf_op jit(solution)/shard_map/pallas_call | solution.py:291
  56.6 2.6 %shard_map.69 = (bf16[192,8192]{1,0:T(8,128)(2,1)}, bf16[8192,128]{1,0:T(8,128)(2,1)}) custom-call(bf16[16,16,144,128]{3,2,1,0:T(8,128)(2,1)S(1)} %get-tuple-element.9.rows, bf16[192,8192]{1,0:T(8,128)(2,1)S(1)} %get-tuple-element.10.keys, bf16[8192,128]{1,0:T(8,128)(2,1)S(1)} %get-tuple-element.11.values, bf16[512,256]{1,0:T(8,128)(2,1)S(1)} %get-tuple-element.12.w, ...), custom_call_target="tpu_custom_call" | custom-call | tf_op jit(solution)/shard_map/pallas_call | solution.py:328

commit v5 on v4

--- a/solution.py
+++ b/solution.py
@@ -44,6 +44,13 @@
         values[pl.ds(at, LANES), :] = part[:, LANES:]
         keys[:LANES, pl.ds(at, LANES)] = part[:, :LANES].T
         keys[LANES:, pl.ds(at, LANES)] = rotary[i].T[: LANES // 2]
+
+
+def falling(part):
+    start, size = 4 * part + RISING[part], 4 - RISING[part]
+    if part < 3:
+        return [(start, size, 12 + part)]
+    return [(start, size - 1, 15), (start + size - 1, 1, 16)]
 
 
 def place_of(source, pair):
@@ -205,8 +212,9 @@
 
             @pl.when(n == 8 + part)
             def _():
-                piece = rows.at[mm, pl.ds(4 * part + count, 4 - count)]
-                downward(piece, piece, 1, m_recv.at[12 + part])
+                for start, size, sem in falling(part):
+                    piece = rows.at[mm, pl.ds(start, size)]
+                    downward(piece, piece, 1, m_recv.at[sem])
 
         @pl.when(n == 2)
         def _():
@@ -235,11 +243,12 @@
     opposite = lax.rem(model + 8, 16)
     for part, count in enumerate(RISING):
         low = rows.at[opposite, pl.ds(4 * part, count)]
-        high = rows.at[opposite, pl.ds(4 * part + count, 4 - count)]
         arrived(count, p_recv.at[12 + part])
         across(low, low, c_recv.at[12 + part])
-        arrived(4 - count, m_recv.at[12 + part])
-        across(high, high, c_recv.at[12 + part])
+        for start, size, sem in falling(part):
+            high = rows.at[opposite, pl.ds(start, size)]
+            arrived(size, m_recv.at[sem])
+            across(high, high, c_recv.at[12 + part])
         if part == 0:
             arrived(8, c_recv.at[11])
             tile(2, 3)
@@ -255,29 +264,25 @@
     send(rows.at[pl.ds(0, 8)], rows.at[pl.ds(0, 8)], c_send, a_recv.at[0], span, other).wait_send()
 
 
-def finish(rows, keys, values, w, gain, keys_hbm, values_hbm, xn, last_keys, last_values, sems):
+def finish(
+    rows, keys_in, values_in, w, gain, keys_hbm, values_hbm, keys, values, xn, sems
+):
     span, model = lax.axis_index("span"), lax.axis_index("model")
     last = (span // 4) ^ 2
     pair = lax.rem(model // 4 + 2, 4)
-    places = [place_of(span ^ mask, pair) for mask in MASKS[12:]]
-
-    def leave(keys_from, k, values_from, v):
-        pltpu.make_async_copy(keys_from, keys_hbm.at[:, k], sems.at[0]).start()
-        pltpu.make_async_copy(values_from, values_hbm.at[v], sems.at[1]).start()
+
+    def leave(part):
+        at = pl.ds(pl.multiple_of(part * 2048, 2048), 2048)
+        pltpu.make_async_copy(keys.at[:, at], keys_hbm.at[:, at], sems.at[0]).start()
+        pltpu.make_async_copy(values.at[at], values_hbm.at[at], sems.at[1]).start()
 
     for i in range(1, 4):
-        at = pl.ds(pl.multiple_of((last ^ i) * 2048, 2048), 2048)
-        leave(keys.at[:, at], at, values.at[at], at)
-    for i in range(4):
-        for other in range(1, 4):
-            at = pl.ds(place_of(last * 4 + i, lax.rem(pair + other, 4)), LANES)
-            leave(keys.at[:, at], at, values.at[at], at)
+        leave(last ^ i)
     expand(
-        rows, pair, range(12, 16), [LANES * i for i in range(4)], gain, w, xn, last_keys, last_values
+        rows, pair, range(12, 16), [place_of(span ^ mask, pair) for mask in MASKS[12:]],
+        gain, w, xn, keys, values,
     )
-    for i in range(4):
-        here, at = pl.ds(LANES * i, LANES), pl.ds(places[i], LANES)
-        leave(last_keys.at[:, here], at, last_values.at[here], at)
+    leave(last)
     pltpu.make_async_copy(keys, keys_hbm, sems.at[0]).wait()
     pltpu.make_async_copy(values, values_hbm, sems.at[1]).wait()
 
@@ -306,7 +311,7 @@
             pltpu.VMEM((len(FAR), TALL, LANES), bf16),
             pltpu.VMEM((len(FAR), TALL, LANES), bf16),
             dma((4,)), dma, dma, dma((2,)), dma,
-            dma((11,)), dma((16,)), dma((16,)), dma((16,)), dma((2,)),
+            dma((11,)), dma((16,)), dma((17,)), dma((16,)), dma((2,)),
             pltpu.SemaphoreType.REGULAR((3,)),
         ],
         compiler_params=pltpu.CompilerParams(
@@ -325,17 +330,13 @@
             )
         )
     )
-    keys, values = pl.pallas_call(
+    keys, values, _, _ = pl.pallas_call(
         finish,
-        out_shape=(keys_shape, values_shape),
+        out_shape=(keys_shape, values_shape) * 2,
         in_specs=[vmem] * 5,
-        out_specs=(hbm, hbm),
-        scratch_shapes=[
-            pltpu.VMEM((512, DEPTH), bf16),
-            pltpu.VMEM((192, 512), bf16),
-            pltpu.VMEM((512, LANES), bf16),
-            dma((2,)),
-        ],
+        out_specs=(hbm, hbm, vmem, vmem),
+        scratch_shapes=[pltpu.VMEM((512, DEPTH), bf16), dma((2,))],
+        input_output_aliases={1: 2, 2: 3},
         compiler_params=pltpu.CompilerParams(vmem_limit_bytes=4 * 1024 * 1024),
     )(*ready)
     return keys.reshape(1, 1, 192, 8192), values.reshape(1, 8192, 1, 128)

time: 59.3 us -> 59.1 us (level)
  no operation moved by 1% of the time
where the time goes in v5:
time: 59.1 us; the launch traced here: 59 us
  Pallas kernels  58.4 us (99%)
  between operations  0.64 us (1%)
    pallas_call x1, Pallas kernels, shards(): pl.pallas_call(exchange, out_shape=(jax.ShapeDtypeStruct((16, 16, TALL, L...  56 us
    pallas_call x1, Pallas kernels, shards(): pl.pallas_call(finish, out_shape=(keys_shape, values_shape) * 2, in_specs...  2.44 us

profile of v5, /device:TPU:1, one launch (start us, length us, event | category | flops | bytes accessed | tf_op | source)
XLA Modules:
  0.0 59.0 jit_solution(6836982137876695194)
XLA Ops:
  0.6 56.0 %shard_map.68 = (bf16[16,16,144,128]{3,2,1,0:T(8,128)(2,1)S(1)}, bf16[192,8192]{1,0:T(8,128)(2,1)S(1)}, bf16[8192,128]{1,0:T(8,128)(2,1)S(1)}, bf16[512,256]{1,0:T(8,128)(2,1)S(1)}, f32[1,512]{1,0:T(1,128)S(1)}) custom-call(bf16[16,32,512]{2,1,0:T(8,128)(2,1)} %lat_hbm.1, bf16[16,32,64]{2,1,0:T(8,128)(2,1)} %rot_hbm.1, f32[1,512]{1,0:T(1,128)} %bitcast.9, ...), custom_call_target="tpu_custom_call" | custom-call | flops 2147483648 | bytes 1048576 | tf_op jit(solution)/shard_map/pallas_call | solution.py:296
  56.6 2.4 %shard_map.69 = (bf16[192,8192]{1,0:T(8,128)(2,1)}, bf16[8192,128]{1,0:T(8,128)(2,1)}, bf16[192,8192]{1,0:T(8,128)(2,1)S(1)}, bf16[8192,128]{1,0:T(8,128)(2,1)S(1)}) custom-call(bf16[16,16,144,128]{3,2,1,0:T(8,128)(2,1)S(1)} %get-tuple-element.9.rows, bf16[192,8192]{1,0:T(8,128)(2,1)S(1)} %get-tuple-element.10.keys_in, ...), custom_call_target="tpu_custom_call", output_to_operand_aliasing={{2}: (1, {}), {3}: (2, {})} | custom-call | tf_op jit(solution)/shard_map/pallas_call | solution.py:333

commit v6 on v5

--- a/solution.py
+++ b/solution.py
@@ -49,8 +49,8 @@
 def falling(part):
     start, size = 4 * part + RISING[part], 4 - RISING[part]
     if part < 3:
-        return [(start, size, 12 + part)]
-    return [(start, size - 1, 15), (start + size - 1, 1, 16)]
+        return [(start, size, 8 + part)]
+    return [(start, size - 1, 11), (start + size - 1, 1, 12)]
 
 
 def place_of(source, pair):
@@ -183,79 +183,95 @@
             gain, w, xn, keys, values,
         )
 
-    @pl.loop(0, 12)
-    def _(n):
-        t, j = n // 4, lax.rem(n, 4)
+    @pl.loop(0, 4)
+    def _(j):
+        below, above = rows.at[down, pl.ds(4 * j, 4)], rows.at[up, pl.ds(4 * j, 4)]
+        arrived(4, p_recv.at[j])
+        upward(below, below, 0, p_recv.at[4 + j // 2])
+        arrived(4, m_recv.at[j])
+        downward(above, above, 0, m_recv.at[4 + j // 2])
+
+        @pl.when(j == 2)
+        def _():
+            arrived(5, a_recv.at[10])
+            for start, count in ((10, 2), (13, 3)):
+                piece = rows.at[model, pl.ds(start, count)]
+                across(piece, piece, c_recv.at[start // 4])
+
+        across(below, below, c_recv.at[j])
+        across(above, above, c_recv.at[j])
+
+        @pl.when(j >= 1)
+        def _():
+            arrived(12, c_recv.at[j - 1])
+            tile(0, j - 1)
+
+    @pl.loop(0, 4)
+    def _(q):
+        t, half = 1 + q // 2, lax.rem(q, 2)
         mp = lax.rem(model + 30 - 2 * t, 16)
         mm = lax.rem(model + 2 + 2 * t, 16)
-        from_below, from_above = rows.at[mp, pl.ds(4 * j, 4)], rows.at[mm, pl.ds(4 * j, 4)]
-        arrived(4, p_recv.at[n])
-
-        @pl.when(t < 2)
-        def _():
-            upward(from_below, from_below, 0, p_recv.at[n + 4])
+        below, above = rows.at[mp, pl.ds(8 * half, 8)], rows.at[mm, pl.ds(8 * half, 8)]
+        arrived(8, p_recv.at[4 + q])
+
+        @pl.when(t == 1)
+        def _():
+            upward(below, below, 0, p_recv.at[6 + half])
 
         for part, count in enumerate(RISING):
 
-            @pl.when(n == 8 + part)
+            @pl.when(q == 2 + part // 2)
             def _():
                 piece = rows.at[mp, pl.ds(4 * part, count)]
-                upward(piece, piece, 1, p_recv.at[12 + part])
-
-        arrived(4, m_recv.at[n])
-
-        @pl.when(t < 2)
-        def _():
-            downward(from_above, from_above, 0, m_recv.at[n + 4])
-
-        for part, count in enumerate(RISING):
-
-            @pl.when(n == 8 + part)
+                upward(piece, piece, 1, p_recv.at[8 + part])
+
+        arrived(8, m_recv.at[4 + q])
+
+        @pl.when(t == 1)
+        def _():
+            downward(above, above, 0, m_recv.at[6 + half])
+
+        for part in range(4):
+
+            @pl.when(q == 2 + part // 2)
             def _():
                 for start, size, sem in falling(part):
                     piece = rows.at[mm, pl.ds(start, size)]
                     downward(piece, piece, 1, m_recv.at[sem])
 
-        @pl.when(n == 2)
-        def _():
-            arrived(5, a_recv.at[10])
-            for start, count in ((10, 2), (13, 3)):
-                piece = rows.at[model, pl.ds(start, count)]
-                across(piece, piece, c_recv.at[start // 4])
-
-        across(from_below, from_below, c_recv.at[n])
-        across(from_above, from_above, c_recv.at[n])
-
-        @pl.when(n >= 1)
-        def _():
-            i = n - 1
-
-            @pl.when(i < 4)
-            def _():
-                arrived(12, c_recv.at[i])
-
-            @pl.when(i >= 4)
-            def _():
-                arrived(8, c_recv.at[i])
-
-            tile(i // 4, lax.rem(i, 4))
+        across(below, below, c_recv.at[4 + q])
+        across(above, above, c_recv.at[4 + q])
+
+        @pl.when(q == 0)
+        def _():
+            arrived(12, c_recv.at[3])
+            tile(0, 3)
+
+        @pl.when(q > 0)
+        def _():
+            arrived(16, c_recv.at[3 + q])
+
+            @pl.loop(0, 2)
+            def _(i):
+                tile((q + 1) // 2, 2 * lax.rem(q - 1, 2) + i)
 
     opposite = lax.rem(model + 8, 16)
     for part, count in enumerate(RISING):
         low = rows.at[opposite, pl.ds(4 * part, count)]
-        arrived(count, p_recv.at[12 + part])
-        across(low, low, c_recv.at[12 + part])
+        arrived(count, p_recv.at[8 + part])
+        across(low, low, c_recv.at[8 + part])
         for start, size, sem in falling(part):
             high = rows.at[opposite, pl.ds(start, size)]
             arrived(size, m_recv.at[sem])
-            across(high, high, c_recv.at[12 + part])
+            across(high, high, c_recv.at[8 + part])
         if part == 0:
-            arrived(8, c_recv.at[11])
+            arrived(16, c_recv.at[7])
+            tile(2, 2)
             tile(2, 3)
         else:
-            arrived(4, c_recv.at[11 + part])
+            arrived(4, c_recv.at[7 + part])
             tile(3, part - 1)
-    arrived(4, c_recv.at[15])
+    arrived(4, c_recv.at[11])
 
     send(pack.at[pl.ds(0, 15)], rows.at[0, pl.ds(0, 15)], a_send, a_recv.at[0], span, other).wait_send()
     send(rows.at[0, pl.ds(0, 10)], rows.at[0, pl.ds(0, 10)], r_send, a_recv.at[0], span, other).wait_send()
@@ -311,7 +327,7 @@
             pltpu.VMEM((len(FAR), TALL, LANES), bf16),
             pltpu.VMEM((len(FAR), TALL, LANES), bf16),
             dma((4,)), dma, dma, dma((2,)), dma,
-            dma((11,)), dma((16,)), dma((17,)), dma((16,)), dma((2,)),
+            dma((11,)), dma((12,)), dma((13,)), dma((12,)), dma((2,)),
             pltpu.SemaphoreType.REGULAR((3,)),
         ],
         compiler_params=pltpu.CompilerParams(

time: 59.1 us -> 59 us (level)
  no operation moved by 1% of the time
where the time goes in v6:
time: 59 us; the launch traced here: 58.9 us
  Pallas kernels  58.3 us (99%)
  between operations  0.64 us (1%)
    pallas_call x1, Pallas kernels, shards(): pl.pallas_call(exchange, out_shape=(jax.ShapeDtypeStruct((16, 16, TALL, L...  55.8 us
    pallas_call x1, Pallas kernels, shards(): pl.pallas_call(finish, out_shape=(keys_shape, values_shape) * 2, in_specs...  2.44 us

profile of v6, /device:TPU:1, one launch (start us, length us, event | category | flops | bytes accessed | tf_op | source)
XLA Modules:
  0.0 58.9 jit_solution(17967535950358169694)
XLA Ops:
  0.6 55.8 %shard_map.68 = (bf16[16,16,144,128]{3,2,1,0:T(8,128)(2,1)S(1)}, bf16[192,8192]{1,0:T(8,128)(2,1)S(1)}, bf16[8192,128]{1,0:T(8,128)(2,1)S(1)}, bf16[512,256]{1,0:T(8,128)(2,1)S(1)}, f32[1,512]{1,0:T(1,128)S(1)}) custom-call(bf16[16,32,512]{2,1,0:T(8,128)(2,1)} %lat_hbm.1, bf16[16,32,64]{2,1,0:T(8,128)(2,1)} %rot_hbm.1, f32[1,512]{1,0:T(1,128)} %bitcast.9, ...), custom_call_target="tpu_custom_call" | custom-call | flops 2147483648 | bytes 1048576 | tf_op jit(solution)/shard_map/pallas_call | solution.py:312
  56.5 2.4 %shard_map.69 = (bf16[192,8192]{1,0:T(8,128)(2,1)}, bf16[8192,128]{1,0:T(8,128)(2,1)}, bf16[192,8192]{1,0:T(8,128)(2,1)S(1)}, bf16[8192,128]{1,0:T(8,128)(2,1)S(1)}) custom-call(bf16[16,16,144,128]{3,2,1,0:T(8,128)(2,1)S(1)} %get-tuple-element.9.rows, bf16[192,8192]{1,0:T(8,128)(2,1)S(1)} %get-tuple-element.10.keys_in, ...), custom_call_target="tpu_custom_call", output_to_operand_aliasing={{2}: (1, {}), {3}: (2, {})} | custom-call | tf_op jit(solution)/shard_map/pallas_call | solution.py:349
